TPU v7x, 32 devices: a whole 2x2x4 slice. The times are simulated.
32 devices in a mesh: fsdp: 8 (over z, core), tp: 4 (over y, x).
Axes of the slice: x: 2, y: 2, z: 4, core: 2. Of those that a mesh axis runs over, the one named last changes fastest.
Arguments:
- hidden: bfloat16 [3072, 7168], P('fsdp'), may hold values from -72 to 72
- w_query: bfloat16 [7168, 4096], P('fsdp', 'tp'), may hold values from -0.0625 to 0.0625
- w_key: bfloat16 [7168, 1024], P('fsdp', 'tp'), may hold values from -0.0625 to 0.0625
- w_value: bfloat16 [7168, 1024], P('fsdp', 'tp'), may hold values from -0.0625 to 0.0625
- w_out: bfloat16 [4096, 7168], P('tp', 'fsdp'), may hold values from -0.09375 to 0.09375
- exp_query: int32 [56, 32], replicated, may hold values from -1 to 1
- exp_key: int32 [56, 8], replicated, may hold values from -1 to 1
- exp_value: int32 [56, 8], replicated, may hold values from -1 to 1
- exp_out: int32 [32, 56], replicated, may hold values from -1 to 1
- owner: int32 [8], replicated, may hold values from 0 to 7, each once
Outputs:
- attended: bfloat16 [3072, 7168], P('fsdp', 'tp')
Inputs may be any that keep to these rules, and one draw needn't show every extreme that they name: Trainer shard i holds logical slab owner[i]; every slab is held once.
All inputs are finite; a program needn't handle non-finite values.
Results may differ from a plain program's by a relative error of at most 0.038.
Values may be sent and summed in bfloat16 or wider, within the bound.
A program may use at most 128 MiB of HBM per device.

v0:
```python
from functools import partial
import math

import jax
import jax.numpy as jnp
from jax import lax
from jax.sharding import PartitionSpec as P

HQ = 32
HK = 8
HD = 128


neg_large = -1e30


def block_factor(exponents, row_start, row_count, col_start, col_count, block_size):
    repeated = jnp.repeat(exponents, block_size, axis=0)
    picked = lax.dynamic_slice_in_dim(repeated, row_start, row_count, 0)
    repeated = jnp.repeat(picked, block_size, axis=1)
    picked = lax.dynamic_slice_in_dim(repeated, col_start, col_count, 1)
    return jnp.exp2(picked.astype(jnp.float32))


def block_update(state, query_half, pos_half, keys_part, values_part, key_pos, inv_root):
    row_max, row_sum, accum = state
    causal = pos_half[:, None] >= key_pos[None, :]
    scores = (
        jnp.einsum("tgjd,ngd->gjtn", query_half, keys_part, preferred_element_type=jnp.float32)
        * inv_root
    )
    scores = jnp.where(causal, scores, neg_large)
    new_max = jnp.maximum(row_max, jnp.max(scores, axis=3))
    rescale = jnp.exp(row_max - new_max)
    weights = jnp.where(causal, jnp.exp(scores - new_max[..., None]), 0.0)
    row_sum = row_sum * rescale + jnp.sum(weights, axis=3)
    accum = accum * rescale[..., None] + jnp.einsum(
        "gjtn,ngd->gjtd",
        weights.astype(jnp.bfloat16),
        values_part,
        preferred_element_type=jnp.float32,
    )
    return (new_max, row_sum, accum)


def keep_state(state):
    return state


def body(hidden, w_query, w_key, w_value, w_out, exp_query, exp_key, exp_value, exp_out, owner):
    fsdp_index = lax.axis_index("fsdp")
    tp_index = lax.axis_index("tp")
    slab_rows = w_query.shape[0]
    groups = owner.shape[0]
    tokens = hidden.shape[0]
    model_width = hidden.shape[1]
    block_size = model_width // exp_query.shape[0]
    slab_start = owner[fsdp_index] * slab_rows
    query_cols = w_query.shape[1]
    key_cols = w_key.shape[1]

    def scaled_rows(weight, exponents):
        col_count = weight.shape[1]
        factor = block_factor(
            exponents, slab_start, slab_rows, tp_index * col_count, col_count, block_size
        )
        return (weight.astype(jnp.float32) * factor).astype(jnp.bfloat16)

    query_local = scaled_rows(w_query, exp_query)
    key_local = scaled_rows(w_key, exp_key)
    value_local = scaled_rows(w_value, exp_value)
    out_rows = w_out.shape[0]
    out_factor = block_factor(
        exp_out, tp_index * out_rows, out_rows, slab_start, slab_rows, block_size
    )
    out_local = (w_out.astype(jnp.float32) * out_factor).astype(jnp.bfloat16)
    arranged = jnp.take(hidden.reshape(tokens, groups, slab_rows), owner, axis=1).reshape(
        tokens, model_width
    )
    pieces = (
        lax.all_gather(query_local, "fsdp", axis=0, tiled=True),
        lax.all_gather(key_local, "fsdp", axis=0, tiled=True),
        lax.all_gather(value_local, "fsdp", axis=0, tiled=True),
    )
    query_sum, key_sum, value_sum = tuple(
        (jnp.dot(arranged, weight, preferred_element_type=jnp.float32) for weight in pieces)
    )
    query = query_sum.astype(jnp.bfloat16)
    key_here = key_sum.astype(jnp.bfloat16)
    value_here = value_sum.astype(jnp.bfloat16)
    half_rows = tokens // 2
    local_pos = fsdp_index * tokens + jnp.arange(tokens, dtype=jnp.int32)
    group_size = HQ // HK
    kv_heads = key_cols // HD
    query_halves = query.reshape(2, half_rows, kv_heads, group_size, HD)
    pos_halves = local_pos.reshape(2, half_rows)
    pos_top = jnp.max(pos_halves, axis=1)
    inv_root = 1.0 / math.sqrt(HD)
    one_state = (
        jnp.full((kv_heads, group_size, half_rows), neg_large, jnp.float32),
        jnp.zeros((kv_heads, group_size, half_rows), jnp.float32),
        jnp.zeros((kv_heads, group_size, half_rows, HD), jnp.float32),
    )
    offset = jnp.int32(0)
    key_piece = lax.all_gather(key_here, "fsdp", axis=0, tiled=True)
    value_piece = lax.all_gather(value_here, "fsdp", axis=0, tiled=True)
    states = list((one_state, one_state))
    piece_rows = key_piece.shape[0]
    for block_low in range(0, piece_rows, 1024):
        block_high = min(block_low + 1024, piece_rows)
        width_here = block_high - block_low
        keys_part = key_piece[block_low:block_high].reshape(width_here, kv_heads, HD)
        values_part = value_piece[block_low:block_high].reshape(width_here, kv_heads, HD)
        key_pos = offset + block_low + jnp.arange(width_here, dtype=jnp.int32)
        for attend_which in range(2):
            update = partial(
                block_update,
                query_half=query_halves[attend_which],
                pos_half=pos_halves[attend_which],
                keys_part=keys_part,
                values_part=values_part,
                key_pos=key_pos,
                inv_root=inv_root,
            )
            states[attend_which] = lax.cond(
                offset + block_low <= pos_top[attend_which],
                update,
                keep_state,
                states[attend_which],
            )
    final_states = tuple(states)
    context_parts = []
    for which in range(2):
        row_max, row_sum, accum = final_states[which]
        part_context = (accum / row_sum[..., None]).astype(jnp.bfloat16)
        context_parts.append(part_context.transpose(2, 0, 1, 3).reshape(half_rows, query_cols))
    context = jnp.concatenate(context_parts, axis=0)
    column_terms = jnp.dot(
        context,
        lax.all_gather(out_local, "fsdp", axis=1, tiled=True),
        preferred_element_type=jnp.float32,
    )
    slab_ids = jnp.arange(groups, dtype=jnp.int32)
    inverse = jnp.sum(
        slab_ids[:, None] * (owner[:, None] == slab_ids[None, :]).astype(jnp.int32), axis=0
    )
    ordered = jnp.take(column_terms.reshape(tokens, groups, slab_rows), inverse, axis=1).reshape(
        tokens, model_width
    )
    result = lax.psum_scatter(ordered.astype(jnp.bfloat16), "tp", scatter_dimension=1, tiled=True)
    return result


def solution(mesh):
    placed = (
        P("fsdp", None),
        P("fsdp", "tp"),
        P("fsdp", "tp"),
        P("fsdp", "tp"),
        P("tp", "fsdp"),
        P(),
        P(),
        P(),
        P(),
        P(),
    )
    return jax.shard_map(
        body, mesh=mesh, in_specs=placed, out_specs=P("fsdp", "tp"), check_vma=False
    )
```

profile of v0, /device:TPU:0, one launch (start us, length us, event | category | flops | bytes accessed | tf_op | source)
XLA Modules:
  0.0 532.7 jit_solution(14240318342266903279)
XLA Ops:
  6.5 1.2 dynamic_slice.27
  8.4 0.8 copy.90
  9.2 0.8 copy.88
  10.6 1.0 broadcast_in_dim.180
  11.6 2.7 copy.224
  14.2 2.1 multiply_convert_fusion.3
  16.5 1.0 broadcast_in_dim.184
  17.5 0.9 copy.223
  18.4 1.0 multiply_convert_fusion.2
  19.4 8.3 %copy.85 = bf16[384,7168]{0,1:T(8,128)(2,1)} copy(bf16[384,7168]{1,0:T(8,128)(2,1)} %param.22) | data formatting | bytes 11010048 | tf_op args[0]
  27.7 8.1 %copy.86 = bf16[384,8,896]{2,0,1:T(8,128)(2,1)} copy(bf16[384,8,896]{0,2,1:T(8,128)(2,1)} %bitcast.184) | data formatting | bytes 11010048 | tf_op jit(solution)/shard_map/reshape | solution.py:77
  35.8 6.3 %gather_fusion = bf16[8,384,896]{2,1,0:T(8,128)(2,1)} fusion(bf16[384,8,896]{2,0,1:T(8,128)(2,1)} %copy.86, s32[1024]{0:T(1024)S(1)} %pad_clamp_fusion.1), kind=kCustom, calls=%fused_computation | custom fusion | bytes 11010080 | tf_op jit(solution)/shard_map/jit(_take)/gather | solution.py:77
  42.1 8.4 %copy.87 = bf16[384,8,896]{0,2,1:T(8,128)(2,1)} copy(bf16[384,8,896]{2,0,1:T(8,128)(2,1)} %bitcast.181) | data formatting | bytes 11010048 | tf_op jit(solution)/shard_map/jit(_take)/gather | solution.py:77
  50.7 7.3 %bitcast_select_fusion.7 = bf16[384,7168]{0,1:T(8,128)(2,1)} fusion(bf16[384,8,896]{0,2,1:T(8,128)(2,1)} %copy.87, pred[7168]{0:T(1024)(128)(4,1)S(1)} %broadcast_in_dim.175), kind=kLoop, calls=%fused_computation.117 | loop fusion | flops 2752512 | bytes 11017216 | tf_op jit(solution)/shard_map/jit(_take)/select_n | solution.py:77
  58.1 3.8 all-gather.7.cloned.1.call-done
  61.8 6.0 %convolution_convert_fusion.2 = bf16[384,256]{1,0:T(8,128)(2,1)} fusion(bf16[384,7168]{0,1:T(8,128)(2,1)} %bitcast_select_fusion.7, bf16[7168,256]{1,0:T(8,128)(2,1)} %all-gather.7.cloned.1.call-done), kind=kOutput, calls=%fused_computation.124 | convolution fusion | flops 1409384448 | bytes 9371648 | tf_op jit(solution)/shard_map/dot_general | solution.py:86
  67.9 37.0 %all-gather.13.cloned.1.call-done = bf16[7168,256]{1,0:T(8,128)(2,1)} async-done(((bf16[896,256]{1,0:T(8,128)(2,1)}), bf16[7168,256]{1,0:T(8,128)(2,1)}) %all-gather.13.cloned.1.call-update) | async-done | bytes 3670032 | tf_op jit(solution)/shard_map/all_gather | solution.py:83
  104.8 6.0 %convolution_convert_fusion.1 = bf16[384,256]{1,0:T(8,128)(2,1)} fusion(bf16[384,7168]{0,1:T(8,128)(2,1)} %bitcast_select_fusion.7, bf16[7168,256]{1,0:T(8,128)(2,1)} %all-gather.13.cloned.1.call-done), kind=kOutput, calls=%fused_computation.123 | convolution fusion | flops 1409384448 | bytes 9371648 | tf_op jit(solution)/shard_map/dot_general | solution.py:86
  111.3 6.4 %broadcast_in_dim.182 = s32[896,32,128]{2,1,0:T(8,128)} broadcast(s32[896,32]{1,0:T(8,128)S(1)} %constant_dynamic-slice_fusion.2), dimensions={0,1} | broadcast | bytes 14794752 | tf_op jit(solution)/shard_map/broadcast_in_dim | solution.py:20
  117.7 25.4 %copy.221 = s32[112,8,32,128]{3,1,2,0:T(8,128)} copy(s32[112,8,32,128]{3,2,1,0:T(8,128)} %bitcast.178) | data formatting | bytes 29360128
  143.1 4.1 multiply_convert_fusion.1
  147.5 8.0 %broadcast_in_dim.186 = s32[1024,56,128]{2,1,0:T(8,128)S(1)} broadcast(s32[1024,56]{1,0:T(8,128)S(1)} %constant_dynamic-slice_fusion), dimensions={0,1} | broadcast | bytes 29589504 | tf_op jit(solution)/shard_map/broadcast_in_dim | solution.py:20
  155.6 13.7 %copy.220 = s32[128,8,56,128]{3,1,2,0:T(8,128)} copy(s32[128,8,56,128]{3,2,1,0:T(8,128)S(1)} %bitcast.177) | data formatting | bytes 58720256
  169.3 4.2 multiply_convert_fusion
  173.7 0.7 fusion.111
  178.4 0.6 broadcast_in_dim.172
  179.0 0.6 pad_clamp_fusion
  179.6 0.6 fusion.110
  180.2 1.5 fusion.108
  181.7 0.9 reshape.158
  182.6 1.5 fusion.107
  184.1 0.9 reshape.163
  185.1 0.9 reshape.165
  186.3 104.8 %all-gather.11.cloned.1.call-done = bf16[7168,1024]{1,0:T(8,128)(2,1)} async-done(((bf16[896,1024]{1,0:T(8,128)(2,1)}), bf16[7168,1024]{1,0:T(8,128)(2,1)}) %all-gather.11.cloned.1.call-update) | async-done | bytes 14680080 | tf_op jit(solution)/shard_map/all_gather | solution.py:81
  291.1 10.7 %convolution_convert_fusion = bf16[384,1024]{1,0:T(8,128)(2,1)S(1)} fusion(bf16[384,7168]{0,1:T(8,128)(2,1)} %bitcast_select_fusion.7, bf16[7168,1024]{1,0:T(8,128)(2,1)} %all-gather.11.cloned.1.call-done), kind=kOutput, calls=%fused_computation.122 | convolution fusion | flops 5637537792 | bytes 20971520 | tf_op jit(solution)/shard_map/dot_general | solution.py:86
  301.9 0.3 squeeze.5
  302.2 9.8 %conditional.9 = (f32[2,4,192]{2,1,0:T(4,128)}, f32[2,4,192]{2,1,0:T(4,128)S(1)}, f32[2,4,192,128]{3,2,1,0:T(8,128)S(1)}) conditional(s32[]{:T(128)} %bitcast.38, () %tuple.52, (s32[1,192]{1,0:T(1,128)S(1)}, s32[1024]{0:T(1024)S(1)}, bf16[1024,2,128]{2,1,0:T(2,128)(2,1)}, bf16[192,2,4,128]{3,2,1,0:T(4,128)(2,1)S(1)}, ...), branch_computations={%region_14.15_spmd, %region_15.18_spmd} | conditional | flops 826152960 | bytes 24058676 | solution.py:125
  302.4 2.5 fusion.49
  304.9 0.6 exponential_multiply_fusion.1
  305.5 2.8 fusion.51
  308.3 0.7 fusion.65
  309.0 2.7 fusion.55
  312.0 0.3 fusion.104
  312.3 0.3 copy.110
  312.6 0.3 reshape.169
  312.9 1.0 squeeze.4
  313.9 15.2 %conditional.6 = (f32[2,4,192]{2,1,0:T(4,128)}, f32[2,4,192]{2,1,0:T(4,128)S(1)}, f32[2,4,192,128]{3,2,1,0:T(8,128)S(1)}) conditional(s32[]{:T(128)} %bitcast.26, () %tuple.47, (s32[1,192]{1,0:T(1,128)}, s32[1024]{0:T(1024)S(1)}, bf16[1024,2,128]{2,1,0:T(2,128)(2,1)}, bf16[192,2,4,128]{3,2,1,0:T(4,128)(2,1)}, bf16[1024,2,128]{2,1,0:T(2,128)(2,1)}) %tuple.147), branch_computations={%region_2.3_spmd, %region_3.6_spmd} | conditional | flops 826152960 | bytes 24058676 | solution.py:125
  318.8 0.9 broadcast_compare_fusion
  319.7 2.6 fusion
  322.3 0.6 exponential_multiply_fusion
  322.9 2.8 fusion.2
  325.7 0.7 fusion.16
  326.4 2.7 fusion.6
  329.1 0.7 copy-done.11
  329.9 0.3 fusion.103
  330.2 0.3 copy.100
  330.8 93.8 %all-gather.17.cloned.1.call-done = bf16[1024,7168]{1,0:T(8,128)(2,1)} async-done(((bf16[1024,896]{1,0:T(8,128)(2,1)}), bf16[1024,7168]{1,0:T(8,128)(2,1)}) %all-gather.17.cloned.1.call-update) | async-done | bytes 14680080 | tf_op jit(solution)/shard_map/all_gather | solution.py:140
  424.6 11.6 %fusion.99 = bf16[384,7168]{1,0:T(8,128)(2,1)S(1)} fusion(bf16[1024,7168]{1,0:T(8,128)(2,1)} %all-gather.17.cloned.1.call-done, bf16[192,1024]{1,0:T(8,128)(2,1)S(1)} %reshape.169, bf16[192,1024]{1,0:T(8,128)(2,1)S(1)} %reshape.168), kind=kOutput, calls=%fused_computation.127 | convolution fusion | flops 5638717440 | bytes 20971520 | tf_op jit(solution)/shard_map/dot_general | solution.py:138
  436.2 3.2 copy.222
  439.5 6.3 %gather_fusion.1 = bf16[8,384,896]{2,1,0:T(8,128)(2,1)} fusion(bf16[384,8,896]{2,0,1:T(8,128)(2,1)} %bitcast.182, s32[1024]{0:T(1024)} %pad_clamp_fusion), kind=kCustom, calls=%fused_computation.1 | custom fusion | bytes 11010080 | tf_op jit(solution)/shard_map/jit(_take)/gather | solution.py:147
  445.7 8.3 %copy.112 = bf16[384,8,896]{0,2,1:T(8,128)(2,1)} copy(bf16[384,8,896]{2,0,1:T(8,128)(2,1)} %bitcast.183) | data formatting | bytes 11010048 | tf_op jit(solution)/shard_map/jit(_take)/gather | solution.py:147
  454.0 7.3 %fusion.98 = bf16[384,7168]{0,1:T(8,128)(2,1)} fusion(bf16[384,8,896]{0,2,1:T(8,128)(2,1)} %copy.112, pred[7168]{0:T(1024)(128)(4,1)S(1)} %copy-done.14), kind=kLoop, calls=%fused_computation.116 | loop fusion | flops 2752512 | bytes 11017216 | tf_op jit(solution)/shard_map/convert_element_type | solution.py:150
  461.4 61.8 %reduce-scatter.2.cloned.1.call-done = bf16[384,1792]{0,1:T(8,128)(2,1)} async-done(((bf16[384,7168]{0,1:T(8,128)(2,1)}), bf16[384,1792]{0,1:T(8,128)(2,1)}) %reduce-scatter.2.cloned.1.call-update) | async-done | bytes 1376272 | tf_op jit(solution)/shard_map/reduce_scatter | solution.py:150
  523.2 2.5 copy.113
  (79 shorter events, 3.0 us)
Async XLA Ops:
  6.5 140.8 %copy-start = (s32[32,56]{1,0:T(8,128)S(1)}, s32[32,56]{1,0:T(8,128)}, u32[]{:S(2)}) copy-start(s32[32,56]{1,0:T(8,128)} %param.30) | copy-start | bytes 21508
  6.5 55.3 %all-gather.7.cloned.1.call-start = ((), (), s32[]{:S(2)}) async-start(), calls=%async_computation.1 | async-start | bytes 4128768 | tf_op jit(solution)/shard_map/all_gather | solution.py:82
  10.5 3.8 copy-start.8
  16.4 2.0 copy-start.9
  16.4 88.4 %all-gather.13.cloned.1.call-start = ((), (), s32[]{:S(2)}) async-start(), calls=%async_computation.4 | async-start | bytes 4128768 | tf_op jit(solution)/shard_map/all_gather | solution.py:83
  19.4 160.9 %all-gather.9.cloned.1.call-start = ((), (), s32[]{:S(2)}) async-start(), calls=%async_computation.2 | async-start | bytes 1769472 | tf_op jit(solution)/shard_map/all_gather | solution.py:105
  27.7 8.1 %copy-start.16 = (s32[8]{0:T(128)S(1)}, s32[8]{0:T(128)}, u32[]{:S(2)}) copy-start(s32[8]{0:T(128)} %param.31) | copy-start | bytes 100
  67.8 43.1 %copy-start.15 = (s32[56,32]{0,1:T(8,128)S(1)}, s32[56,32]{0,1:T(8,128)}, u32[]{:S(2)}) copy-start(s32[56,32]{0,1:T(8,128)} %param.27) | copy-start | bytes 21508
  67.8 114.8 %all-gather.15.cloned.1.call-start = ((), (), s32[]{:S(2)}) async-start(), calls=%async_computation.5 | async-start | bytes 1769472 | tf_op jit(solution)/shard_map/all_gather | solution.py:106
  110.9 180.2 %all-gather.11.cloned.1.call-start = ((), (), s32[]{:S(2)}) async-start(), calls=%async_computation.3 | async-start | bytes 16515072 | tf_op jit(solution)/shard_map/all_gather | solution.py:81
  117.7 25.4 %copy-start.2 = (bf16[896,1024]{1,0:T(8,128)(2,1)S(1)}, bf16[896,1024]{1,0:T(8,128)(2,1)}, u32[]{:S(2)}) copy-start(bf16[896,1024]{1,0:T(8,128)(2,1)} %param.23) | copy-start | bytes 5505028
  147.3 277.4 %all-gather.17.cloned.1.call-start = ((), (), s32[]{:S(2)}) async-start(), calls=%async_computation.6 | async-start | bytes 16515072 | tf_op jit(solution)/shard_map/all_gather | solution.py:140
  155.6 13.7 %copy-start.3 = (bf16[1024,896]{1,0:T(8,128)(2,1)S(1)}, bf16[1024,896]{1,0:T(8,128)(2,1)}, u32[]{:S(2)}) copy-start(bf16[1024,896]{1,0:T(8,128)(2,1)} %param.26) | copy-start | bytes 5505028
  173.5 349.7 %reduce-scatter.2.cloned.1.call-start = ((), (), s32[]{:S(2)}) async-start(), calls=%async_computation.7 | async-start | bytes 6881280 | tf_op jit(solution)/shard_map/reduce_scatter | solution.py:150
  179.0 132.9 %copy-start.12 = (s32[1024]{0:T(1024)}, s32[1024]{0:T(1024)S(1)}, u32[]{:S(2)}) copy-start(s32[1024]{0:T(1024)S(1)} %iota_add_fusion.1) | copy-start | bytes 12292
  179.0 132.9 %copy-start.10 = (s32[1024]{0:T(1024)}, s32[1024]{0:T(1024)S(1)}, u32[]{:S(2)}) copy-start(s32[1024]{0:T(1024)S(1)} %iota_add_fusion) | copy-start | bytes 12292
  302.4 6.6 %copy-start.6 = (bf16[1024,2,128]{2,1,0:T(2,128)(2,1)S(1)}, bf16[1024,2,128]{2,1,0:T(2,128)(2,1)}, u32[]{:S(2)}) copy-start(bf16[1024,2,128]{2,1,0:T(2,128)(2,1)} %get-tuple-element.334) | copy-start | bytes 1572868 | tf_op jit(solution)/shard_map/cond
  313.9 15.2 %copy-start.4 = (bf16[1024,2,128]{2,1,0:T(2,128)(2,1)S(1)}, bf16[1024,2,128]{2,1,0:T(2,128)(2,1)}, u32[]{:S(2)}) copy-start(bf16[1024,2,128]{2,1,0:T(2,128)(2,1)} %reshape.165) | copy-start | bytes 1572868
  313.9 15.2 %copy-start.13 = (s32[1024]{0:T(1024)S(1)}, s32[1024]{0:T(1024)}, u32[]{:S(2)}) copy-start(s32[1024]{0:T(1024)} %copy-done.12) | copy-start | bytes 12292
  319.7 6.7 %copy-start.7 = (bf16[1024,2,128]{2,1,0:T(2,128)(2,1)S(1)}, bf16[1024,2,128]{2,1,0:T(2,128)(2,1)}, u32[]{:S(2)}) copy-start(bf16[1024,2,128]{2,1,0:T(2,128)(2,1)} %get-tuple-element.313) | copy-start | bytes 1572868 | tf_op jit(solution)/shard_map/cond
  329.1 0.7 copy-start.11
  445.7 8.3 %copy-start.14 = (pred[7168]{0:T(1024)(128)(4,1)S(1)}, pred[7168]{0:T(1024)(128)(4,1)}, u32[]{:S(2)}) copy-start(pred[7168]{0:T(1024)(128)(4,1)} %broadcast_in_dim.172) | copy-start | bytes 21508
  454.0 71.7 %copy-start.1 = (s32[32,56]{1,0:T(8,128)S(1)}, s32[32,56]{1,0:T(8,128)}, u32[]{:S(2)}) copy-start(s32[32,56]{1,0:T(8,128)} %param.30) | copy-start | bytes 21508
Sparse Core Ops, SparseCore 0:
  16.5 45.2 all-gather.6
  63.5 41.3 all-gather.12
  106.5 24.0 all-gather.8
  132.1 24.3 all-gather.14
  158.0 133.0 all-gather.10
  292.5 132.0 all-gather.16
  461.5 61.6 reduce-scatter.1
where the time goes:
time: 543 us; the launch traced here: 533 us
  waiting for transfers between devices  301 us (55%)
  local copies, waits for them, and re-layouts  126 us (23%)
  matrix products  44.8 us (8%)
  other arithmetic  36.7 us (7%)
  between operations  18.7 us (3%)
    all_gather x1, waiting for transfers between devices, body(): lax.all_gather(query_local, 'fsdp', axis=0, tiled=True)  105 us
    all_gather x1, waiting for transfers between devices, body(): lax.all_gather(out_local, 'fsdp', axis=1, tiled=True)  93.8 us
    reduce_scatter x1, waiting for transfers between devices, body(): lax.psum_scatter(ordered.astype(jnp.bfloat16), 'tp', scatter_dimension=1,...  61.8 us
    unnamed x36, local copies, waits for them, and re-layouts  53.3 us
    all_gather x1, waiting for transfers between devices, body(): lax.all_gather(value_local, 'fsdp', axis=0, tiled=True)  37 us
    dot_general x3, matrix products, body(): jnp.dot(arranged, weight, preferred_element_type=jnp.float32)  22.7 us
    broadcast_in_dim x4, local copies, waits for them, and re-layouts, block_factor(): repeated = jnp.repeat(picked, block_size, axis=1)  16.5 us
    gather x2, local copies, waits for them, and re-layouts, body(): jnp.take(hidden.reshape(tokens, groups, slab_rows), owner, axis=1)  14.7 us
  transfers between devices with their start and end apart: 7, of which 5 were waited for; matrix products, arithmetic and copies ran while one was open for 30% of the time, Pallas kernels for 0%

commit v1 on v0

--- a/solution.py
+++ b/solution.py
@@ -4,6 +4,8 @@
 import jax
 import jax.numpy as jnp
 from jax import lax
+from jax.experimental import pallas as pl
+from jax.experimental.pallas import tpu as pltpu
 from jax.sharding import PartitionSpec as P
 
 HQ = 32
@@ -47,7 +49,7 @@
     return state
 
 
-def body(hidden, w_query, w_key, w_value, w_out, exp_query, exp_key, exp_value, exp_out, owner):
+def gather_body(hidden, w_query, w_key, w_value, w_out, exp_query, exp_key, exp_value, exp_out, owner):
     fsdp_index = lax.axis_index("fsdp")
     tp_index = lax.axis_index("tp")
     slab_rows = w_query.shape[0]
@@ -151,7 +153,374 @@
     return result
 
 
+MESH = pl.DeviceIdType.MESH
+VMEM = pltpu.VMEM
+
+
+def greet(peers):
+    barrier = pltpu.get_barrier_semaphore()
+    for device in peers:
+        pl.semaphore_signal(barrier, inc=1, device_id=device, device_id_type=MESH)
+    pl.semaphore_wait(barrier, len(peers))
+
+
+def near_first(n):
+    steps = []
+    for d in range(1, n // 2 + 1):
+        steps.append(d)
+        if n - d != d:
+            steps.append(n - d)
+    return steps
+
+
+def spread_kernel(n_f, n_t, piece_ref, out_ref, send_one, send_two, recv, local_sem):
+    f = lax.axis_index("fsdp")
+    t = lax.axis_index("tp")
+    far = [lax.rem(f + d, n_f) for d in range(n_f)]
+    side = [lax.rem(t + k, n_t) for k in range(n_t)]
+    greet([{"fsdp": far[d]} for d in range(1, n_f)] + [{"tp": side[k]} for k in range(1, n_t)])
+    own = pltpu.make_async_copy(piece_ref.at[f], out_ref.at[f, t], local_sem)
+    own.start()
+    copies = []
+    order = near_first(n_f)
+    for d in order:
+        copies.append(
+            pltpu.make_async_remote_copy(
+                src_ref=piece_ref.at[far[d]],
+                dst_ref=out_ref.at[f, t],
+                send_sem=send_one.at[d],
+                recv_sem=recv.at[f, t],
+                device_id={"fsdp": far[d]},
+                device_id_type=MESH,
+            )
+        )
+        copies[-1].start()
+
+    def forward(slot, source, from_f):
+        for k in range(1, n_t):
+            copies.append(
+                pltpu.make_async_remote_copy(
+                    src_ref=source,
+                    dst_ref=out_ref.at[from_f, t],
+                    send_sem=send_two.at[slot, k],
+                    recv_sem=recv.at[from_f, t],
+                    device_id={"tp": side[k]},
+                    device_id_type=MESH,
+                )
+            )
+            copies[-1].start()
+
+    def arrived(from_f, from_t):
+        pltpu.make_async_remote_copy(
+            src_ref=piece_ref.at[0],
+            dst_ref=out_ref.at[from_f, from_t],
+            send_sem=send_one.at[0],
+            recv_sem=recv.at[from_f, from_t],
+            device_id={"tp": side[1]},
+            device_id_type=MESH,
+        ).wait_recv()
+
+    forward(0, piece_ref.at[f], f)
+    for d in order:
+        source = lax.rem(f - d + n_f, n_f)
+        arrived(source, t)
+        forward(d, out_ref.at[source, t], source)
+    for d in [0] + order:
+        for k in range(1, n_t):
+            arrived(lax.rem(f - d + n_f, n_f), lax.rem(t - k + n_t, n_t))
+    for copy in copies:
+        copy.wait_send()
+    own.wait()
+
+
+def spread(pieces, n_f, n_t):
+    _, rows, cols = pieces.shape
+    return pl.pallas_call(
+        partial(spread_kernel, n_f, n_t),
+        out_shape=jax.ShapeDtypeStruct((n_f, n_t, rows, cols), pieces.dtype),
+        in_specs=[pl.BlockSpec(memory_space=VMEM)],
+        out_specs=pl.BlockSpec(memory_space=VMEM),
+        scratch_shapes=[
+            pltpu.SemaphoreType.DMA((n_f,)),
+            pltpu.SemaphoreType.DMA((n_f, n_t)),
+            pltpu.SemaphoreType.DMA((n_f, n_t)),
+            pltpu.SemaphoreType.DMA,
+        ],
+        compiler_params=pltpu.CompilerParams(collective_id=0, has_side_effects=True),
+        name="spread_hidden",
+    )(pieces)
+
+
+def exchange_kernel(n, axis, piece_ref, out_ref, send, recv, local_sem):
+    me = lax.axis_index(axis)
+    peers = [lax.rem(me + d, n) for d in range(n)]
+    greet([{axis: peers[d]} for d in range(1, n)])
+    own = pltpu.make_async_copy(piece_ref.at[me], out_ref.at[me], local_sem)
+    own.start()
+    copies = []
+    for d in near_first(n):
+        copies.append(
+            pltpu.make_async_remote_copy(
+                src_ref=piece_ref.at[peers[d]],
+                dst_ref=out_ref.at[me],
+                send_sem=send.at[d],
+                recv_sem=recv.at[me],
+                device_id={axis: peers[d]},
+                device_id_type=MESH,
+            )
+        )
+        copies[-1].start()
+    for d in near_first(n):
+        source = lax.rem(me - d + n, n)
+        pltpu.make_async_remote_copy(
+            src_ref=piece_ref.at[0],
+            dst_ref=out_ref.at[source],
+            send_sem=send.at[0],
+            recv_sem=recv.at[source],
+            device_id={axis: peers[1]},
+            device_id_type=MESH,
+        ).wait_recv()
+    for copy in copies:
+        copy.wait_send()
+    own.wait()
+
+
+def exchange(pieces, n, axis, collective_id):
+    return pl.pallas_call(
+        partial(exchange_kernel, n, axis),
+        out_shape=jax.ShapeDtypeStruct(pieces.shape, pieces.dtype),
+        in_specs=[pl.BlockSpec(memory_space=VMEM)],
+        out_specs=pl.BlockSpec(memory_space=VMEM),
+        scratch_shapes=[
+            pltpu.SemaphoreType.DMA((n,)),
+            pltpu.SemaphoreType.DMA((n,)),
+            pltpu.SemaphoreType.DMA,
+        ],
+        compiler_params=pltpu.CompilerParams(collective_id=collective_id, has_side_effects=True),
+        name="exchange_" + axis,
+    )(pieces)
+
+
+def scale_into(out_ref, w_ref, fac_ref, at, blocks, block):
+    for b in range(blocks):
+        rows = slice(b * block, (b + 1) * block)
+        for c in range(0, w_ref.shape[1], block):
+            cols = slice(at + c, at + c + block)
+            weight = w_ref[rows, c : c + block].astype(jnp.float32)
+            out_ref[rows, cols] = (weight * fac_ref[b : b + 1, cols]).astype(jnp.bfloat16)
+
+
+def project_kernel(heads, kv_heads, share, block, h_ref, wq_ref, wk_ref, wv_ref, fac_ref, out_ref, w_scr):
+    q_cols = wq_ref.shape[1]
+    k_cols = wk_ref.shape[1]
+    blocks = wq_ref.shape[0] // block
+
+    @pl.when(pl.program_id(0) == 0)
+    def _():
+        scale_into(w_scr, wq_ref, fac_ref, 0, blocks, block)
+        scale_into(w_scr, wk_ref, fac_ref, q_cols, blocks, block)
+        scale_into(w_scr, wv_ref, fac_ref, q_cols + k_cols, blocks, block)
+
+    rows = h_ref.shape[0]
+    part = rows // share
+    both = jnp.dot(h_ref[...], w_scr[:, :], preferred_element_type=jnp.float32).astype(jnp.bfloat16)
+    for j in range(heads):
+        g, p = j // share, j % share
+        out_ref[j, 0, :rows, :] = both[:, j * HD : (j + 1) * HD]
+        span = slice(p * part, (p + 1) * part)
+        k_at = q_cols + g * HD
+        v_at = q_cols + k_cols + g * HD
+        out_ref[j, 0, rows : rows + part, :] = both[span, k_at : k_at + HD]
+        out_ref[j, 0, rows + part :, :] = both[span, v_at : v_at + HD]
+
+
+def attend_kernel(inv_root, key_rows, q_ref, k_ref, v_ref, out_ref):
+    i = pl.program_id(0)
+    rows = q_ref.shape[0]
+    query = q_ref[...]
+
+    def step(j, state, masked):
+        row_max, row_sum, accum = state
+        at = pl.ds(pl.multiple_of(j * key_rows, key_rows), key_rows)
+        scores = (
+            lax.dot_general(
+                query, k_ref[at, :], (((1,), (1,)), ((), ())), preferred_element_type=jnp.float32
+            )
+            * inv_root
+        )
+        if masked:
+            q_pos = lax.broadcasted_iota(jnp.int32, scores.shape, 0)
+            k_pos = lax.broadcasted_iota(jnp.int32, scores.shape, 1)
+            scores = jnp.where(q_pos >= k_pos, scores, neg_large)
+        new_max = jnp.maximum(row_max, jnp.max(scores, axis=1, keepdims=True))
+        rescale = jnp.exp(row_max - new_max)
+        weights = jnp.exp(scores - new_max)
+        row_sum = row_sum * rescale + jnp.sum(weights, axis=1, keepdims=True)
+        accum = accum * rescale + jnp.dot(
+            weights.astype(jnp.bfloat16), v_ref[at, :], preferred_element_type=jnp.float32
+        )
+        return (new_max, row_sum, accum)
+
+    state = (
+        jnp.full((rows, 1), neg_large, jnp.float32),
+        jnp.zeros((rows, 1), jnp.float32),
+        jnp.zeros((rows, HD), jnp.float32),
+    )
+    state = step(i, state, True)
+    _, row_sum, accum = lax.fori_loop(0, i, lambda j, s: step(j, s, False), state)
+    out_ref[...] = (accum / row_sum).astype(jnp.bfloat16)
+
+
+def out_kernel(heads, block, n_t, c_ref, w_ref, fac_ref, out_ref, w_scr):
+    blocks = w_ref.shape[0] // block
+
+    @pl.when(pl.program_id(0) == 0)
+    def _():
+        w_scr[...] = jnp.zeros_like(w_scr)
+        scale_into(w_scr, w_ref, fac_ref, 0, blocks, block)
+
+    context = jnp.concatenate([c_ref[h] for h in range(heads)], axis=1)
+    part = jnp.dot(context, w_scr[...], preferred_element_type=jnp.float32).astype(jnp.bfloat16)
+    quarter, slab = out_ref.shape[2], out_ref.shape[3]
+    for r in range(n_t):
+        out_ref[r, 0, :, :] = part[r * quarter : (r + 1) * quarter, :slab]
+
+
+def stationary_body(
+    n_f, n_t, hidden, w_query, w_key, w_value, w_out, exp_query, exp_key, exp_value, exp_out, owner
+):
+    f = lax.axis_index("fsdp")
+    t = lax.axis_index("tp")
+    here, width = hidden.shape
+    slab = w_query.shape[0]
+    tokens = here * n_f
+    block = width // exp_query.shape[0]
+    slab_blocks = slab // block
+    q_cols, k_cols = w_query.shape[1], w_key.shape[1]
+    heads, kv_heads = q_cols // HD, k_cols // HD
+    share = heads // kv_heads
+    quarter = here // n_t
+    logical = owner[f]
+
+    def factors(exponents, cols):
+        picked = lax.dynamic_slice(
+            exponents, (logical * slab_blocks, t * (cols // block)), (slab_blocks, cols // block)
+        )
+        return jnp.repeat(jnp.exp2(picked.astype(jnp.float32)), block, axis=1)
+
+    in_factor = jnp.concatenate(
+        [factors(exp_query, q_cols), factors(exp_key, k_cols), factors(exp_value, k_cols)], axis=1
+    )
+    out_rows = w_out.shape[0] // block
+    out_factor = jnp.repeat(
+        jnp.exp2(
+            lax.dynamic_slice(
+                exp_out, (t * out_rows, logical * slab_blocks), (out_rows, slab_blocks)
+            ).astype(jnp.float32)
+        ),
+        block,
+        axis=1,
+    )
+
+    in_factor = jnp.pad(in_factor, ((0, -slab_blocks % 8), (0, 0)))
+    out_factor = jnp.pad(out_factor, ((0, -out_rows % 8), (0, -slab % 256)))
+
+    mine = lax.dynamic_slice_in_dim(hidden, t * quarter, quarter, 0)
+    pieces = jnp.stack(
+        [lax.dynamic_slice_in_dim(mine, owner[i] * slab, slab, 1) for i in range(n_f)]
+    )
+    arranged = spread(pieces, n_f, n_t).reshape(tokens, slab)
+
+    steps = share
+    rows = tokens // steps
+    part = rows // share
+    whole = lambda a: pl.BlockSpec(a.shape, lambda i: (0,) * a.ndim)
+    packed = pl.pallas_call(
+        partial(project_kernel, heads, kv_heads, share, block),
+        grid=(steps,),
+        out_shape=jax.ShapeDtypeStruct((heads, steps, rows + 2 * part, HD), jnp.bfloat16),
+        in_specs=[
+            pl.BlockSpec((rows, slab), lambda i: (i, 0)),
+            whole(w_query),
+            whole(w_key),
+            whole(w_value),
+            whole(in_factor),
+        ],
+        out_specs=pl.BlockSpec((heads, 1, rows + 2 * part, HD), lambda i: (0, i, 0, 0)),
+        scratch_shapes=[pltpu.VMEM((slab, q_cols + 2 * k_cols), jnp.bfloat16)],
+        compiler_params=pltpu.CompilerParams(vmem_limit_bytes=56 * 1024 * 1024),
+        name="project",
+    )(arranged, w_query, w_key, w_value, in_factor)
+    summed = lax.psum_scatter(packed, "fsdp", scatter_dimension=0, tiled=False)
+
+    groups = [[g * share + p for p in range(share)] for g in range(kv_heads)]
+    kv = lax.all_gather(
+        summed[:, rows:, :].reshape(steps, 2, part, HD),
+        "fsdp",
+        axis=1,
+        tiled=False,
+        axis_index_groups=groups,
+    )
+    kv = kv.transpose(2, 0, 1, 3, 4).reshape(2, tokens, HD)
+    query = summed[:, :rows, :].reshape(tokens, HD)
+    tile = here
+    context = pl.pallas_call(
+        partial(attend_kernel, 1.0 / math.sqrt(HD), tile),
+        grid=(tokens // tile,),
+        out_shape=jax.ShapeDtypeStruct((tokens, HD), jnp.bfloat16),
+        in_specs=[
+            pl.BlockSpec((tile, HD), lambda i: (i, 0)),
+            pl.BlockSpec((pl.squeezed, tokens, HD), lambda i: (0, 0, 0)),
+            pl.BlockSpec((pl.squeezed, tokens, HD), lambda i: (1, 0, 0)),
+        ],
+        out_specs=pl.BlockSpec((tile, HD), lambda i: (i, 0)),
+        compiler_params=pltpu.CompilerParams(vmem_limit_bytes=48 * 1024 * 1024),
+        name="attend",
+    )(query, kv, kv)
+
+    gathered = lax.all_gather(context, "fsdp", axis=0, tiled=False)
+    parts = pl.pallas_call(
+        partial(out_kernel, heads, block, n_t),
+        grid=(n_f,),
+        out_shape=jax.ShapeDtypeStruct((n_t, n_f, quarter, slab), jnp.bfloat16),
+        in_specs=[
+            pl.BlockSpec((heads, here, HD), lambda i: (0, i, 0)),
+            whole(w_out),
+            whole(out_factor),
+        ],
+        out_specs=pl.BlockSpec((n_t, 1, quarter, slab), lambda i: (0, i, 0, 0)),
+        scratch_shapes=[pltpu.VMEM((w_out.shape[0], slab + -slab % 256), jnp.bfloat16)],
+        compiler_params=pltpu.CompilerParams(vmem_limit_bytes=48 * 1024 * 1024),
+        name="project_out",
+    )(gathered, w_out, out_factor)
+    total = lax.psum_scatter(parts, "tp", scatter_dimension=0, tiled=False)
+
+    by_slab = exchange(total, n_f, "fsdp", 1)
+    slab_ids = jnp.arange(n_f, dtype=jnp.int32)
+    inverse = jnp.sum(
+        slab_ids[:, None] * (owner[:, None] == slab_ids[None, :]).astype(jnp.int32), axis=0
+    )
+    per = n_f // n_t
+    columns = jnp.stack(
+        [
+            jnp.concatenate([by_slab[inverse[r * per + c]] for c in range(per)], axis=1)
+            for r in range(n_t)
+        ]
+    )
+    return exchange(columns, n_t, "tp", 2).reshape(here, width // n_t)
+
+
 def solution(mesh):
+    n_f, n_t = mesh.shape["fsdp"], mesh.shape["tp"]
+
+    def body(*arrays):
+        hidden, w_query, w_key = arrays[0], arrays[1], arrays[2]
+        heads, kv_heads = w_query.shape[1] // HD, w_key.shape[1] // HD
+        fits = heads == n_f and n_f % n_t == 0 and hidden.shape[0] % (16 * n_t) == 0
+        if fits:
+            return stationary_body(n_f, n_t, *arrays)
+        return gather_body(*arrays)
+
     placed = (
         P("fsdp", None),
         P("fsdp", "tp"),

time: 543 us -> 466 us (0.86); the launches traced: 533 us -> 465 us
  Pallas kernels: 0 us -> 177 us
  local copies, waits for them, and re-layouts: 126 us -> 20.8 us
  waiting for transfers between devices: 301 us -> 228 us
  matrix products: 44.8 us -> 0 us
  other arithmetic: 36.7 us -> 4.43 us
  between operations: 18.7 us -> 34 us
    pallas_call x0 -> x6, Pallas kernels: none -> 177 us  [the longest x1 71.6 us: spread(): pl.pallas_call(partial(spread_kernel, n_f, n_t), out_shape=jax.ShapeDtype...]
    all_gather x6 -> x2, waiting for transfers between devices: 239 us -> 84.5 us  [the longest x1 64 us: stationary_body(): gathered = lax.all_gather(context, 'fsdp', axis=0, tiled=False)]
    unnamed x7 -> x5, waiting for transfers between devices: 0.11 us -> 45.9 us
    dot_general x8 -> x0, matrix products: 44.8 us -> none  [the longest x3 22.7 us: body(): jnp.dot(arranged, weight, preferred_element_type=jnp.float32)]
    unnamed x36 -> x24, local copies, waits for them, and re-layouts: 53.3 us -> 13.4 us
    reduce_scatter x1, waiting for transfers between devices: 61.8 us -> 98 us  [stationary_body(): summed = lax.psum_scatter(packed, 'fsdp', scatter_dimension=0, tiled=False)]
    gather x4 -> x0, local copies, waits for them, and re-layouts: 29.2 us -> none  [the longest x2 14.7 us: body(): jnp.take(hidden.reshape(tokens, groups, slab_rows), owner, axis=1)]
    convert_element_type x5 -> x0, other arithmetic: 18.7 us -> none  [the longest x1 7.31 us: body(): ordered.astype(jnp.bfloat16)]
  transfers between devices with their start and end apart: 7 -> 4, of which waited for: 5 -> 4; matrix products, arithmetic and copies ran while one was open for 30% -> 0% of each run, Pallas kernels for 0% -> 0%
where the time goes in v1:
time: 466 us; the launch traced here: 465 us
  waiting for transfers between devices  228 us (49%)
  Pallas kernels  177 us (38%)
  between operations  34 us (7%)
  local copies, waits for them, and re-layouts  20.8 us (4%)
    reduce_scatter x1, waiting for transfers between devices, stationary_body(): summed = lax.psum_scatter(packed, 'fsdp', scatter_dimension=0, tiled=False)  98 us
    pallas_call x1, Pallas kernels, spread(): pl.pallas_call(partial(spread_kernel, n_f, n_t), out_shape=jax.ShapeDtype...  71.6 us
    all_gather x1, waiting for transfers between devices, stationary_body(): gathered = lax.all_gather(context, 'fsdp', axis=0, tiled=False)  64 us
    pallas_call x2, Pallas kernels, exchange(): pl.pallas_call(partial(exchange_kernel, n, axis), out_shape=jax.ShapeDtyp...  58.1 us
    unnamed x5, waiting for transfers between devices  45.9 us
    pallas_call x1, Pallas kernels, stationary_body(): pl.pallas_call(partial(attend_kernel, 1.0 / math.sqrt(HD), tile), grid=(t...  21.1 us
    all_gather x1, waiting for transfers between devices, stationary_body(): lax.all_gather(summed[:, rows:, :].reshape(steps, 2, part, HD), 'fsdp', a...  20.5 us
    pallas_call x1, Pallas kernels, stationary_body(): pl.pallas_call(partial(project_kernel, heads, kv_heads, share, block), gr...  14.6 us
  transfers between devices with their start and end apart: 4, of which 4 were waited for; matrix products, arithmetic and copies ran while one was open for 0% of the time, Pallas kernels for 0%

profile of v1, /device:TPU:0, one launch (start us, length us, event | category | flops | bytes accessed | tf_op | source)
XLA Modules:
  0.0 464.9 jit_solution(13685600665894538457)
XLA Ops:
  6.5 0.0 reduce-scatter.5.cloned.1.call-start
  6.5 1.7 fusion.1
  13.2 1.1 bitcast_dynamic-update-slice_fusion.7
  14.3 1.1 bitcast_dynamic-update-slice_fusion.6
  15.4 1.1 bitcast_dynamic-update-slice_fusion.5
  16.5 1.1 bitcast_dynamic-update-slice_fusion.4
  17.5 1.1 bitcast_dynamic-update-slice_fusion.3
  18.6 1.1 bitcast_dynamic-update-slice_fusion.2
  19.7 1.1 bitcast_dynamic-update-slice_fusion.1
  20.8 1.1 bitcast_dynamic-update-slice_fusion.piece_ref
  21.9 0.0 copy-start.2
  21.9 1.1 copy-done.2
  22.9 71.6 %spread_hidden.1 = bf16[8,4,96,896]{3,2,1,0:T(8,128)(2,1)} custom-call(bf16[8,96,896]{2,1,0:T(8,128)(2,1)} %copy-done.2), custom_call_target="tpu_custom_call" | custom-call | tf_op jit(solution)/shard_map/spread_hidden/pallas_call | solution.py:238
  95.2 0.8 multiply_exponential_fusion.1
  96.0 0.1 copy.21
  96.1 0.1 broadcast_bitcast_fusion.1
  96.2 0.8 multiply_exponential_fusion.2
  96.9 0.1 copy.23
  97.0 0.1 broadcast_bitcast_fusion.2
  97.1 0.1 copy.22
  97.2 0.1 broadcast_bitcast_fusion.3
  97.3 0.6 select_maximum_fusion.fac_ref
  97.9 14.6 %project.1 = bf16[8,4,1152,128]{3,2,1,0:T(8,128)(2,1)} custom-call(bf16[3072,896]{1,0:T(8,128)(2,1)} %bitcast.88, bf16[896,1024]{1,0:T(8,128)(2,1)} %wq_ref.1, bf16[896,256]{1,0:T(8,128)(2,1)} %wk_ref.1, bf16[896,256]{1,0:T(8,128)(2,1)} %wv_ref.1, f32[8,1536]{1,0:T(8,128)} %select_maximum_fusion.fac_ref), custom_call_target="tpu_custom_call" | custom-call | tf_op jit(solution)/shard_map/project/pallas_call | solution.py:438
  112.5 0.0 reduce-scatter.5.cloned.1.call-update
  112.6 0.0 all-gather.4.cloned.1.call-start
  112.6 98.0 %reduce-scatter.5.cloned.1.call-done = bf16[1,4,1152,128]{3,2,1,0:T(8,128)(2,1)} async-done(((bf16[8,4,1152,128]{3,2,1,0:T(8,128)(2,1)}), bf16[1,4,1152,128]{3,2,1,0:T(8,128)(2,1)}) %reduce-scatter.5.cloned.1.call-update) | async-done | bytes 1179664 | tf_op jit(solution)/shard_map/reduce_scatter | solution.py:454
  210.6 0.0 copy-start.3
  210.6 1.1 slice.73
  211.7 0.8 copy.24
  212.5 0.0 all-gather.4.cloned.1.call-update
  212.5 0.0 all-gather.6.cloned.1.call-start
  212.5 0.0 copy-done.3
  212.6 0.1 slice.72
  212.6 20.5 %all-gather.4.cloned.1.call-done = bf16[4,4,2,192,128]{4,3,1,0,2:T(8,128)(2,1)} async-done(((bf16[4,1,2,192,128]{4,3,1,0,2:T(8,128)(2,1)}), bf16[4,4,2,192,128]{4,3,1,0,2:T(8,128)(2,1)}) %all-gather.4.cloned.1.call-update) | async-done | bytes 1572880 | tf_op jit(solution)/shard_map/all_gather | solution.py:457
  233.1 0.0 copy-start
  233.1 1.4 copy-done
  234.5 0.0 copy-start.1
  234.5 21.1 %attend.1 = bf16[3072,128]{1,0:T(8,128)(2,1)} custom-call(bf16[3072,128]{1,0:T(8,128)(2,1)S(1)} %bitcast.87, bf16[2,3072,128]{2,1,0:T(8,128)(2,1)S(1)} %bitcast.85, bf16[2,3072,128]{2,1,0:T(8,128)(2,1)S(1)} %bitcast.86), custom_call_target="tpu_custom_call" | custom-call | tf_op jit(solution)/shard_map/attend/pallas_call | solution.py:467
  255.6 0.0 all-gather.6.cloned.1.call-update
  255.7 0.0 reduce-scatter.7.cloned.1.call-start
  255.7 0.8 multiply_exponential_fusion
  256.5 0.1 copy.25
  256.6 0.1 broadcast_bitcast_fusion
  256.6 64.0 %all-gather.6.cloned.1.call-done = bf16[24576,128]{1,0:T(8,128)(2,1)} async-done(((bf16[3072,128]{1,0:T(8,128)(2,1)}), bf16[24576,128]{1,0:T(8,128)(2,1)}) %all-gather.6.cloned.1.call-update) | async-done | bytes 6291472 | tf_op jit(solution)/shard_map/all_gather | solution.py:481
  320.6 0.0 copy-done.1
  320.6 11.9 %project_out.1 = bf16[4,8,96,896]{3,2,1,0:T(8,128)(2,1)} custom-call(bf16[8,3072,128]{2,1,0:T(8,128)(2,1)} %bitcast.89, bf16[1024,896]{1,0:T(8,128)(2,1)S(1)} %copy-done.1, f32[8,1024]{1,0:T(8,128)S(1)} %pad.9.fac_ref), custom_call_target="tpu_custom_call" | custom-call | tf_op jit(solution)/shard_map/project_out/pallas_call | solution.py:482
  332.5 0.0 copy-start.4
  332.5 0.0 reduce-scatter.7.cloned.1.call-update
  332.6 0.6 copy-done.4
  333.2 0.1 select_reduce_fusion
  333.3 0.7 fusion
  349.1 45.8 %reduce-scatter.7.cloned.1.call-done = bf16[1,8,96,896]{3,2,1,0:T(8,128)(2,1)} async-done(((bf16[4,8,96,896]{3,2,1,0:T(8,128)(2,1)}), bf16[1,8,96,896]{3,2,1,0:T(8,128)(2,1)}) %reduce-scatter.7.cloned.1.call-update) | async-done | bytes 1376272
  394.9 37.1 %exchange_fsdp.1 = bf16[8,96,896]{2,1,0:T(8,128)(2,1)} custom-call(bf16[8,96,896]{2,1,0:T(8,128)(2,1)} %bitcast.92), custom_call_target="tpu_custom_call" | custom-call | tf_op jit(solution)/shard_map/exchange_fsdp/pallas_call | solution.py:289
  432.0 1.5 dynamic-slice_bitcast_fusion.7
  433.7 1.3 pad_maximum_fusion.piece_ref
  434.9 21.0 %exchange_tp.1 = bf16[4,96,1792]{2,1,0:T(8,128)(2,1)} custom-call(bf16[4,96,1792]{2,1,0:T(8,128)(2,1)} %pad_maximum_fusion.piece_ref), custom_call_target="tpu_custom_call" | custom-call | tf_op jit(solution)/shard_map/exchange_tp/pallas_call | solution.py:289
  455.9 2.5 copy.43
  (8 shorter events, 0.1 us)
Async XLA Ops:
  6.5 204.0 %reduce-scatter.5.cloned.1.call-start = ((), (), s32[]{:S(2)}) async-start(), calls=%async_computation.2 | async-start | bytes 10616832 | tf_op jit(solution)/shard_map/reduce_scatter | solution.py:454
  21.9 1.1 copy-start.2
  112.6 120.6 %all-gather.4.cloned.1.call-start = ((), (), s32[]{:S(2)}) async-start(), calls=%async_computation.3 | async-start | bytes 1966080 | tf_op jit(solution)/shard_map/all_gather | solution.py:457
  210.6 2.0 copy-start.3
  212.5 108.1 %all-gather.6.cloned.1.call-start = ((), (), s32[]{:S(2)}) async-start(), calls=%async_computation.4 | async-start | bytes 7077888 | tf_op jit(solution)/shard_map/all_gather | solution.py:481
  233.1 1.4 copy-start
  234.5 86.1 %copy-start.1 = (bf16[1024,896]{1,0:T(8,128)(2,1)S(1)}, bf16[1024,896]{1,0:T(8,128)(2,1)}, u32[]{:S(2)}) copy-start(bf16[1024,896]{1,0:T(8,128)(2,1)} %w_ref.1) | copy-start | bytes 5505028
  255.7 139.2 %reduce-scatter.7.cloned.1.call-start = ((), (), s32[]{:S(2)}) async-start(), calls=%async_computation.5 | async-start | bytes 6881280
  332.5 0.7 copy-start.4
Sparse Core Ops, SparseCore 0:
  112.7 97.8 reduce-scatter.4
  212.6 20.4 all-gather.3
  255.8 64.8 all-gather.5
  332.7 62.1 reduce-scatter.6
